TPU v7x, 32 devices: a whole 2x2x4 slice. The times are simulated.
32 devices in a mesh: rows: 4 (over x, core), cols: 8 (over z, y).
Axes of the slice: x: 2, y: 2, z: 4, core: 2. Of those that a mesh axis runs over, the one named last changes fastest.
Arguments:
- design: bfloat16 [4096, 8192], P('rows', 'cols'), may hold values from -6 to 6
- theta: float32 [8192], P('cols'), may hold values from -0.0625 to 0.0625
- feature_scale: float32 [8192], P('cols'), may hold values from 0.05 to 2
- labels: int32 [4096], P('rows'), may hold values 0 or 1
- psi: bfloat16 [1024, 256], replicated, may hold values from -0.1875 to 0.1875
- phi: float32 [512, 256], replicated, may hold values from -0.25 to 0.25
Outputs:
- newton_step: float32 [8192], P('cols')
- sketch: float32 [256, 8192], P(None, 'cols')
All inputs are finite; a program needn't handle non-finite values. No bound on the sum of `labels` on one device may be relied on, other than what follows from the above.
Results may differ from a plain program's by a relative error of at most 0.0085.
Values sent between devices are 32-bit elements; how exact they have to be, the bound alone decides.
A program may use at most 128 MiB of HBM per device.

v0:
```python
import jax
import jax.numpy as jnp
from jax import lax
from jax.sharding import PartitionSpec as P

ITERS = 10


damping = 0.01
shrink_share = 0.05
highest = lax.Precision.HIGHEST


def swapped(value, axis, stride):
    mask = 2**stride
    pairs = [(source, source ^ mask) for source in range(lax.axis_size(axis))]
    return lax.ppermute(value, axis, pairs)


def shrink_weights(range_rows):
    width = range_rows.shape[1]
    moment = jnp.dot(range_rows.T, range_rows, precision=highest)
    ridge = shrink_share * jnp.trace(moment) / width
    factor = jnp.linalg.cholesky(moment + ridge * jnp.eye(width, dtype=jnp.float32))
    return jax.scipy.linalg.solve_triangular(factor, range_rows.T, lower=True)


def on_device(design, theta, feature_scale, labels, psi, phi):
    row_devices = lax.axis_size("rows")
    samples = design.shape[0] * row_devices
    width = psi.shape[1]
    scaled_theta = (theta * feature_scale).astype(jnp.bfloat16)
    margins = lax.psum(jnp.dot(design, scaled_theta, preferred_element_type=jnp.float32), "cols")
    chance = jax.nn.sigmoid(margins)
    weight = chance * (1.0 - chance)
    misfit = (chance - labels.astype(jnp.float32)).astype(jnp.bfloat16)
    summed_grad = lax.psum(jnp.dot(misfit, design, preferred_element_type=jnp.float32), "rows")
    gradient = feature_scale * summed_grad / samples + damping * theta
    rows_scaled = (
        design.astype(jnp.float32) * jnp.sqrt(weight)[:, None] * feature_scale[None, :]
    ).astype(jnp.bfloat16)
    mixed_cols = jnp.einsum(
        "rf,rs->fs", rows_scaled, psi, preferred_element_type=jnp.float32
    ).astype(jnp.bfloat16)
    range_rows = lax.psum(
        jnp.dot(rows_scaled, mixed_cols, preferred_element_type=jnp.float32), "cols"
    )
    leaf_weights = shrink_weights(range_rows).astype(jnp.bfloat16)
    sketch = jnp.dot(leaf_weights, rows_scaled, preferred_element_type=jnp.float32)
    position = lax.axis_index("rows")
    for level_bit in range(row_devices.bit_length() - 1):
        partner = swapped(sketch, "rows", level_bit)
        first_low = position // (1 << level_bit) % 2 == 0
        lower_half = jnp.where(first_low, sketch, partner)
        upper_half = jnp.where(first_low, partner, sketch)
        stacked = jnp.concatenate([lower_half, upper_half], 0)
        gram = lax.psum(jnp.dot(stacked, stacked.T, precision=highest), "cols")
        range_rows = jnp.dot(gram, phi, precision=highest)
        sketch = jnp.dot(shrink_weights(range_rows), stacked, precision=highest)
    kernel_part = lax.psum(jnp.dot(sketch, sketch.T, precision=highest), "cols")
    kernel = kernel_part + damping * samples * jnp.eye(width, dtype=jnp.float32)
    kernel_factor = jnp.linalg.cholesky(kernel)
    solution = jnp.zeros_like(gradient)
    residual = gradient

    def precondition_plus(vector):
        projected, squared = lax.psum(
            (jnp.dot(sketch, vector, precision=highest), jnp.sum(vector * vector)), "cols"
        )
        solved = jax.scipy.linalg.cho_solve((kernel_factor, True), projected)
        smoothed = (vector - jnp.dot(solved, sketch, precision=highest)) / damping
        return (smoothed, (squared - jnp.sum(projected * solved)) / damping)

    search, agreement = precondition_plus(residual)
    for turn_index in range(ITERS):
        rounded = (feature_scale * search).astype(jnp.bfloat16)
        forward_rows, length = lax.psum(
            (
                jnp.dot(design, rounded, preferred_element_type=jnp.float32),
                jnp.sum(search * search),
            ),
            "cols",
        )
        inner = (weight * forward_rows).astype(jnp.bfloat16)
        back_sum, bending = lax.psum(
            (
                jnp.dot(inner, design, preferred_element_type=jnp.float32),
                jnp.sum(forward_rows * inner.astype(jnp.float32)),
            ),
            "rows",
        )
        product = feature_scale * back_sum / samples + damping * search
        product, curvature = (product, bending / samples + damping * length)
        step_size = agreement / curvature
        solution = solution + step_size * search
        residual = residual - step_size * product
        if turn_index + 1 < ITERS:
            smoothed, agreement_next = precondition_plus(residual)
            search = smoothed + agreement_next / agreement * search
            agreement = agreement_next
    return (solution, sketch)


def solution(mesh):
    in_specs = (P("rows", "cols"), P("cols"), P("cols"), P("rows"), P(), P())
    out_specs = (P("cols"), P(None, "cols"))
    return jax.shard_map(
        on_device, mesh=mesh, in_specs=in_specs, out_specs=out_specs, check_vma=False
    )
```

profile of v0, /device:TPU:0, one launch (start us, length us, event | category | flops | bytes accessed | tf_op | source)
XLA Modules:
  0.0 1238.0 jit_solution(12997754419069925355)
XLA Ops:
  10.4 23.2 %psum.455 = f32[1024]{0:T(1024)S(1)} all-reduce(f32[1024]{0:T(1024)S(1)} %bitcast.779), channel_id=1, replica_groups=mesh['rows'=4,'cols'=8] {'cols'}, use_global_device_ids=true, to_apply=%region_0.0 | all-reduce | flops 1024 | bytes 8192 | tf_op jit(solution)/shard_map/psum | solution.py:33
  37.7 75.0 %all-reduce.34.cloned.1.call-done = f32[1024,256]{1,0:T(8,128)} async-done(((f32[1024,256]{1,0:T(8,128)}), f32[1024,256]{1,0:T(8,128)}) %all-reduce.34.cloned.1.call-update) | async-done | bytes 1048592 | tf_op jit(solution)/shard_map/psum | solution.py:45
  158.9 19.7 %custom-call.20 = f32[2,128,128]{1,2,0:T(8,128)S(1)} custom-call(f32[2,128,128]{2,1,0:T(8,128)S(1)} %get-tuple-element.28), custom_call_target="InvertDiagBlocksLowerTriangular" | custom-call | tf_op jit(solution)/shard_map/jit(_solve_triangular)/triangular_solve | solution.py:25
  195.9 77.6 %all-reduce.36.cloned.1.call-done = f32[512,512]{1,0:T(8,128)} async-done(((f32[512,512]{1,0:T(8,128)}), f32[512,512]{1,0:T(8,128)}) %all-reduce.36.cloned.1.call-update) | async-done | bytes 1048592 | tf_op jit(solution)/shard_map/psum | solution.py:57
  306.8 11.8 cholesky.265
  328.4 20.5 %custom-call.36 = f32[2,128,128]{1,2,0:T(8,128)S(1)} custom-call(f32[2,128,128]{2,1,0:T(8,128)} %copy-done.15), custom_call_target="InvertDiagBlocksLowerTriangular" | custom-call | tf_op jit(solution)/shard_map/jit(_solve_triangular)/triangular_solve | solution.py:25
  355.9 23.7 %collective-permute-done.1 = f32[256,1024]{1,0:T(8,128)} collective-permute-done((f32[256,1024]{1,0:T(8,128)}, f32[256,1024]{1,0:T(8,128)}, u32[]{:S(2)}, u32[]{:S(2)}) %collective-permute-start.1) | collective-permute-done | bytes 1048608 | tf_op jit(solution)/shard_map/ppermute | solution.py:17
  393.5 71.1 %all-reduce.38.cloned.1.call-done = f32[512,512]{1,0:T(8,128)} async-done(((f32[512,512]{1,0:T(8,128)}), f32[512,512]{1,0:T(8,128)}) %all-reduce.38.cloned.1.call-update) | async-done | bytes 1048592 | tf_op jit(solution)/shard_map/psum | solution.py:57
  498.0 12.1 cholesky.299
  519.8 20.5 %custom-call.38 = f32[2,128,128]{1,2,0:T(8,128)S(1)} custom-call(f32[2,128,128]{2,1,0:T(8,128)} %copy-done.16), custom_call_target="InvertDiagBlocksLowerTriangular" | custom-call | tf_op jit(solution)/shard_map/jit(_solve_triangular)/triangular_solve | solution.py:25
  550.4 20.2 %psum.461 = f32[256]{0:T(256)S(1)} all-reduce(f32[256]{0:T(256)S(1)} %bitcast.781), channel_id=1, replica_groups=mesh['rows'=4,'cols'=8] {'cols'}, use_global_device_ids=true, to_apply=%region_13.16 | all-reduce | flops 256 | bytes 2048 | tf_op jit(solution)/shard_map/psum | solution.py:67
  570.7 47.8 %all-reduce.40.cloned.1.call-done = f32[256,256]{0,1:T(8,128)} async-done(((f32[256,256]{0,1:T(8,128)}), f32[256,256]{0,1:T(8,128)}) %all-reduce.40.cloned.1.call-update) | async-done | bytes 262160 | tf_op jit(solution)/shard_map/psum | solution.py:60
  662.5 19.9 %custom-call.40 = f32[2,128,128]{1,2,0:T(8,128)S(1)} custom-call(f32[2,128,128]{2,1,0:T(8,128)S(1)} %get-tuple-element.91), custom_call_target="InvertDiagBlocksLowerTriangular" | custom-call | tf_op jit(solution)/shard_map/jit(_cho_solve)/triangular_solve | solution.py:70
  686.6 20.6 %all-reduce.19 = (f32[1024]{0:T(1024)S(1)}, f32[]{:T(128)}, f32[]{:T(128)}) all-reduce(f32[1024]{0:T(1024)S(1)} %bitcast.760, f32[]{:T(128)} %get-tuple-element.250, f32[]{:T(128)} %get-tuple-element.248), channel_id=1, replica_groups=mesh['rows'=4,'cols'=8] {'cols'}, use_global_device_ids=true, to_apply=%region_17.21 | all-reduce | flops 1026 | bytes 8208 | tf_op jit(solution)/shard_map/psum | solution.py:77
  720.7 17.8 %all-reduce.18 = (f32[256]{0:T(256)S(1)}, f32[]{:T(128)}) all-reduce(f32[256]{0:T(256)S(1)} %bitcast.792, f32[]{:T(128)} %get-tuple-element.244), channel_id=1, replica_groups=mesh['rows'=4,'cols'=8] {'cols'}, use_global_device_ids=true, to_apply=%region_25.29 | all-reduce | flops 257 | bytes 2056 | tf_op jit(solution)/shard_map/psum | solution.py:67
  744.7 20.0 %all-reduce.17 = (f32[1024]{0:T(1024)S(1)}, f32[]{:T(128)}) all-reduce(f32[1024]{0:T(1024)S(1)} %bitcast.762, f32[]{:T(128)} %get-tuple-element.242), channel_id=1, replica_groups=mesh['rows'=4,'cols'=8] {'cols'}, use_global_device_ids=true, to_apply=%region_27.31 | all-reduce | flops 1025 | bytes 8200 | tf_op jit(solution)/shard_map/psum | solution.py:77
  776.3 17.8 %all-reduce.16 = (f32[256]{0:T(256)S(1)}, f32[]{:T(128)}) all-reduce(f32[256]{0:T(256)S(1)} %bitcast.793, f32[]{:T(128)} %get-tuple-element.238), channel_id=1, replica_groups=mesh['rows'=4,'cols'=8] {'cols'}, use_global_device_ids=true, to_apply=%region_35.39 | all-reduce | flops 257 | bytes 2056 | tf_op jit(solution)/shard_map/psum | solution.py:67
  800.3 20.0 %all-reduce.15 = (f32[1024]{0:T(1024)S(1)}, f32[]{:T(128)}) all-reduce(f32[1024]{0:T(1024)S(1)} %bitcast.764, f32[]{:T(128)} %get-tuple-element.236), channel_id=1, replica_groups=mesh['rows'=4,'cols'=8] {'cols'}, use_global_device_ids=true, to_apply=%region_37.41 | all-reduce | flops 1025 | bytes 8200 | tf_op jit(solution)/shard_map/psum | solution.py:77
  831.9 18.2 %all-reduce.14 = (f32[256]{0:T(256)S(1)}, f32[]{:T(128)}) all-reduce(f32[256]{0:T(256)S(1)} %bitcast.794, f32[]{:T(128)} %get-tuple-element.232), channel_id=1, replica_groups=mesh['rows'=4,'cols'=8] {'cols'}, use_global_device_ids=true, to_apply=%region_45.49 | all-reduce | flops 257 | bytes 2056 | tf_op jit(solution)/shard_map/psum | solution.py:67
  858.0 20.0 %all-reduce.13 = (f32[1024]{0:T(1024)S(1)}, f32[]{:T(128)}) all-reduce(f32[1024]{0:T(1024)S(1)} %bitcast.766, f32[]{:T(128)} %get-tuple-element.230), channel_id=1, replica_groups=mesh['rows'=4,'cols'=8] {'cols'}, use_global_device_ids=true, to_apply=%region_47.51 | all-reduce | flops 1025 | bytes 8200 | tf_op jit(solution)/shard_map/psum | solution.py:77
  889.5 17.8 %all-reduce.12 = (f32[256]{0:T(256)S(1)}, f32[]{:T(128)}) all-reduce(f32[256]{0:T(256)S(1)} %bitcast.795, f32[]{:T(128)} %get-tuple-element.226), channel_id=1, replica_groups=mesh['rows'=4,'cols'=8] {'cols'}, use_global_device_ids=true, to_apply=%region_55.59 | all-reduce | flops 257 | bytes 2056 | tf_op jit(solution)/shard_map/psum | solution.py:67
  915.2 20.0 %all-reduce.11 = (f32[1024]{0:T(1024)S(1)}, f32[]{:T(128)}) all-reduce(f32[1024]{0:T(1024)S(1)} %bitcast.768, f32[]{:T(128)} %get-tuple-element.224), channel_id=1, replica_groups=mesh['rows'=4,'cols'=8] {'cols'}, use_global_device_ids=true, to_apply=%region_57.61 | all-reduce | flops 1025 | bytes 8200 | tf_op jit(solution)/shard_map/psum | solution.py:77
  946.8 17.8 %all-reduce.10 = (f32[256]{0:T(256)S(1)}, f32[]{:T(128)}) all-reduce(f32[256]{0:T(256)S(1)} %bitcast.796, f32[]{:T(128)} %get-tuple-element.220), channel_id=1, replica_groups=mesh['rows'=4,'cols'=8] {'cols'}, use_global_device_ids=true, to_apply=%region_65.69 | all-reduce | flops 257 | bytes 2056 | tf_op jit(solution)/shard_map/psum | solution.py:67
  972.5 20.0 %all-reduce.9 = (f32[1024]{0:T(1024)S(1)}, f32[]{:T(128)}) all-reduce(f32[1024]{0:T(1024)S(1)} %bitcast.770, f32[]{:T(128)} %get-tuple-element.218), channel_id=1, replica_groups=mesh['rows'=4,'cols'=8] {'cols'}, use_global_device_ids=true, to_apply=%region_67.71 | all-reduce | flops 1025 | bytes 8200 | tf_op jit(solution)/shard_map/psum | solution.py:77
  1004.0 17.8 %all-reduce.8 = (f32[256]{0:T(256)S(1)}, f32[]{:T(128)}) all-reduce(f32[256]{0:T(256)S(1)} %bitcast.797, f32[]{:T(128)} %get-tuple-element.214), channel_id=1, replica_groups=mesh['rows'=4,'cols'=8] {'cols'}, use_global_device_ids=true, to_apply=%region_75.79 | all-reduce | flops 257 | bytes 2056 | tf_op jit(solution)/shard_map/psum | solution.py:67
  1029.8 20.0 %all-reduce.7 = (f32[1024]{0:T(1024)S(1)}, f32[]{:T(128)}) all-reduce(f32[1024]{0:T(1024)S(1)} %bitcast.772, f32[]{:T(128)} %get-tuple-element.212), channel_id=1, replica_groups=mesh['rows'=4,'cols'=8] {'cols'}, use_global_device_ids=true, to_apply=%region_77.81 | all-reduce | flops 1025 | bytes 8200 | tf_op jit(solution)/shard_map/psum | solution.py:77
  1061.4 17.9 %all-reduce.6 = (f32[256]{0:T(256)S(1)}, f32[]{:T(128)}) all-reduce(f32[256]{0:T(256)S(1)} %bitcast.798, f32[]{:T(128)} %get-tuple-element.208), channel_id=1, replica_groups=mesh['rows'=4,'cols'=8] {'cols'}, use_global_device_ids=true, to_apply=%region_85.89 | all-reduce | flops 257 | bytes 2056 | tf_op jit(solution)/shard_map/psum | solution.py:67
  1087.3 20.0 %all-reduce.5 = (f32[1024]{0:T(1024)S(1)}, f32[]{:T(128)}) all-reduce(f32[1024]{0:T(1024)S(1)} %bitcast.774, f32[]{:T(128)} %get-tuple-element.206), channel_id=1, replica_groups=mesh['rows'=4,'cols'=8] {'cols'}, use_global_device_ids=true, to_apply=%region_87.91 | all-reduce | flops 1025 | bytes 8200 | tf_op jit(solution)/shard_map/psum | solution.py:77
  1118.9 17.8 %all-reduce.4 = (f32[256]{0:T(256)S(1)}, f32[]{:T(128)}) all-reduce(f32[256]{0:T(256)S(1)} %bitcast.799, f32[]{:T(128)} %get-tuple-element.202), channel_id=1, replica_groups=mesh['rows'=4,'cols'=8] {'cols'}, use_global_device_ids=true, to_apply=%region_95.99 | all-reduce | flops 257 | bytes 2056 | tf_op jit(solution)/shard_map/psum | solution.py:67
  1144.6 20.0 %all-reduce.3 = (f32[1024]{0:T(1024)S(1)}, f32[]{:T(128)}) all-reduce(f32[1024]{0:T(1024)S(1)} %bitcast.776, f32[]{:T(128)} %get-tuple-element.200), channel_id=1, replica_groups=mesh['rows'=4,'cols'=8] {'cols'}, use_global_device_ids=true, to_apply=%region_97.101 | all-reduce | flops 1025 | bytes 8200 | tf_op jit(solution)/shard_map/psum | solution.py:77
  1176.3 17.8 %all-reduce.2 = (f32[256]{0:T(256)S(1)}, f32[]{:T(128)}) all-reduce(f32[256]{0:T(256)S(1)} %bitcast.800, f32[]{:T(128)} %get-tuple-element.196), channel_id=1, replica_groups=mesh['rows'=4,'cols'=8] {'cols'}, use_global_device_ids=true, to_apply=%region_105.109 | all-reduce | flops 257 | bytes 2056 | tf_op jit(solution)/shard_map/psum | solution.py:67
  1202.1 20.0 %all-reduce.1 = (f32[1024]{0:T(1024)S(1)}, f32[]{:T(128)}) all-reduce(f32[1024]{0:T(1024)S(1)} %bitcast.778, f32[]{:T(128)} %get-tuple-element.194), channel_id=1, replica_groups=mesh['rows'=4,'cols'=8] {'cols'}, use_global_device_ids=true, to_apply=%region_107.111 | all-reduce | flops 1025 | bytes 8200 | tf_op jit(solution)/shard_map/psum | solution.py:77
  (370 shorter events, 405.9 us)
Async XLA Ops:
  7.2 26.4 %copy-start = (bf16[1024,256]{1,0:T(8,128)(2,1)S(1)}, bf16[1024,256]{1,0:T(8,128)(2,1)}, u32[]{:S(2)}) copy-start(bf16[1024,256]{1,0:T(8,128)(2,1)} %param.15) | copy-start | bytes 1572868
  7.2 26.4 %copy-start.10 = (f32[1024]{0:T(1024)S(1)}, f32[1024]{0:T(1024)}, u32[]{:S(2)}) copy-start(f32[1024]{0:T(1024)} %param.13) | copy-start | bytes 12292
  7.2 26.4 %copy-start.1 = (bf16[1024,1024]{1,0:T(8,128)(2,1)S(1)}, bf16[1024,1024]{1,0:T(8,128)(2,1)}, u32[]{:S(2)}) copy-start(bf16[1024,1024]{1,0:T(8,128)(2,1)} %param.11) | copy-start | bytes 6291460
  7.2 26.3 %copy-start.18 = (s32[1024]{0:T(1024)S(1)}, s32[1024]{0:T(1024)}, u32[]{:S(2)}) copy-start(s32[1024]{0:T(1024)} %param.14) | copy-start | bytes 12292
  7.2 105.5 %all-reduce.34.cloned.1.call-start = ((), (), s32[]{:S(2)}) async-start(), calls=%async_computation | async-start | bytes 2097152 | tf_op jit(solution)/shard_map/psum | solution.py:45
  36.9 236.5 %all-reduce.36.cloned.1.call-start = ((), (), s32[]{:S(2)}) async-start(), calls=%async_computation.1 | async-start | bytes 2097152 | tf_op jit(solution)/shard_map/psum | solution.py:57
  158.9 19.7 %copy-start.19 = (s32[2,2]{1,0:T(2,128)}, s32[2,2]{1,0:T(2,128)S(1)}, u32[]{:S(2)}) copy-start(s32[2,2]{1,0:T(2,128)S(1)} %get-tuple-element.492) | copy-start | bytes 52
  184.9 3.0 collective-permute-start
  189.6 1.0 copy-start.7
  189.6 1.3 copy-start.9
  195.4 269.2 %all-reduce.38.cloned.1.call-start = ((), (), s32[]{:S(2)}) async-start(), calls=%async_computation.2 | async-start | bytes 2097152 | tf_op jit(solution)/shard_map/psum | solution.py:57
  281.7 0.7 copy-start.13
  318.7 2.6 copy-start.11
  327.7 0.6 copy-start.15
  348.9 1.5 copy-start.8
  354.5 25.2 %collective-permute-start.1 = (f32[256,1024]{1,0:T(8,128)}, f32[256,1024]{1,0:T(8,128)}, u32[]{:S(2)}, u32[]{:S(2)}) collective-permute-start(f32[256,1024]{1,0:T(8,128)} %fusion.2), channel_id=1, source_target_pairs={{0,16},{8,24},{16,0},{24,8},{1,17},{9,25},{17,1},{25,9},{2,18},{10... | collective-permute-start | bytes 3145736 | tf_op jit(solution)/shard_map/ppermute | solution.py:17
  381.3 1.0 copy-start.4
  381.3 1.3 copy-start.6
  387.2 231.2 %all-reduce.40.cloned.1.call-start = ((), (), s32[]{:S(2)}) async-start(), calls=%async_computation.3 | async-start | bytes 524288 | tf_op jit(solution)/shard_map/psum | solution.py:60
  472.9 0.7 copy-start.14
  510.1 2.6 copy-start.12
  519.1 0.6 copy-start.16
  540.3 1.5 copy-start.5
  544.9 1.0 copy-start.2
  545.8 1.8 copy-start.17
  662.5 132.4 %copy-start.3 = (f32[256,256]{1,0:T(8,128)}, f32[256,256]{1,0:T(8,128)S(1)}, u32[]{:S(2)}) copy-start(f32[256,256]{1,0:T(8,128)S(1)} %get-tuple-element.476) | copy-start | bytes 786436
Sparse Core Ops, SparseCore 0:
  37.0 75.6 all-reduce.33
  195.6 77.8 all-reduce.35
  387.3 77.2 all-reduce.37
  547.7 70.6 all-reduce.39
where the time goes:
time: 1240 us
  blocking collectives  475 us (38%)
  waiting for transfers between devices  298 us (24%)
  other arithmetic  259 us (21%)
  matrix products  123 us (10%)
  between operations  48.3 us (4%)
  local copies, waits for them, and re-layouts  32.1 us (3%)
    psum x10, blocking collectives, on_device(): lax.psum((jnp.dot(design, rounded, preferred_element_type=jnp.float32), j...  201 us
    psum x10, blocking collectives, precondition_plus(): lax.psum((jnp.dot(sketch, vector, precision=highest), jnp.sum(vector * ve...  181 us
    psum x2, waiting for transfers between devices, on_device(): gram = lax.psum(jnp.dot(stacked, stacked.T, precision=highest), 'cols')  149 us
    another operation x20, other arithmetic, shrink_weights(): jnp.linalg.cholesky(moment + ridge * jnp.eye(width, dtype=jnp.float32))  105 us
    psum x1, waiting for transfers between devices, on_device(): lax.psum(jnp.dot(rows_scaled, mixed_cols, preferred_element_type=jnp.floa...  75 us
    psum x10, blocking collectives, on_device(): lax.psum((jnp.dot(inner, design, preferred_element_type=jnp.float32), jnp...  64.5 us
    another operation x7, other arithmetic, shrink_weights(): return jax.scipy.linalg.solve_triangular(factor, range_rows.T, lower=True)  63.2 us
    psum x1, waiting for transfers between devices, on_device(): kernel_part = lax.psum(jnp.dot(sketch, sketch.T, precision=highest), 'cols')  47.8 us
  transfers between devices with their start and end apart: 6, of which 6 were waited for; matrix products, arithmetic and copies ran while one was open for 0% of the time, Pallas kernels for 0%

commit v1 on v0

v1 whole, which is shorter than its diff:
```python
import functools

import jax
import jax.numpy as jnp
from jax import lax
from jax.experimental import pallas as pl
from jax.experimental.pallas import tpu as pltpu
from jax.sharding import PartitionSpec as P

ITERS = 10
BLOCK = 32
LANES = 128

damping = 0.01
shrink_share = 0.05
highest = lax.Precision.HIGHEST
MESH = pl.DeviceIdType.MESH
VMEM_SPEC = pl.BlockSpec(memory_space=pltpu.VMEM)
f32 = jnp.float32
bf16 = jnp.bfloat16


def iota(shape, axis):
    return lax.broadcasted_iota(jnp.int32, shape, axis)


def split3(value):
    high = value.astype(bf16)
    rest = value - high.astype(f32)
    mid = rest.astype(bf16)
    low = (rest - mid.astype(f32)).astype(bf16)
    return high, mid, low


def nn(a, b, precision=None):
    return lax.dot_general(a, b, (((1,), (0,)), ((), ())), precision=precision, preferred_element_type=f32)


def nt(a, b, precision=None):
    return lax.dot_general(a, b, (((1,), (1,)), ((), ())), precision=precision, preferred_element_type=f32)


def tn(a, b, precision=None):
    return lax.dot_general(a, b, (((0,), (0,)), ((), ())), precision=precision, preferred_element_type=f32)


def inverse_factor(work, out, width):
    def block_step(b, carry):
        start = pl.multiple_of(b * BLOCK, BLOCK)
        rows = work[pl.ds(start, BLOCK), :]
        left = rows[:, :width]
        shifted = pltpu.roll(left, width - start, 1)[:, :LANES]
        lane = iota((BLOCK, LANES), 1)
        sub = iota((BLOCK, LANES), 0)
        small = jnp.where(lane < BLOCK, shifted, jnp.where(lane == sub + BLOCK, 1.0, 0.0))
        diag = jnp.ones((BLOCK, 1), f32)
        mixing = jnp.zeros((BLOCK, 1), f32)
        sub1 = iota((BLOCK, 1), 0)
        for j in range(0, BLOCK, 2):
            col0, col1 = small[:, j : j + 1], small[:, j + 1 : j + 2]
            row0, row1 = small[j : j + 1, :], small[j + 1 : j + 2, :]
            p00 = small[j : j + 1, j : j + 1]
            p01 = small[j : j + 1, j + 1 : j + 2]
            p11 = small[j + 1 : j + 2, j + 1 : j + 2]
            det = p00 * p11 - p01 * p01
            diag = jnp.where(sub1 == j, p00, jnp.where(sub1 == j + 1, det / p00, diag))
            mixing = jnp.where(sub1 == j + 1, p01 / p00, mixing)
            if j + 2 < BLOCK:
                share = 1.0 / det
                new0 = (p11 * row0 - p01 * row1) * share
                new1 = (p00 * row1 - p01 * row0) * share
                below0 = jnp.where(sub1 > j + 1, col0, 0.0)
                below1 = jnp.where(sub1 > j + 1, col1, 0.0)
                small = small - below0 * new0 - below1 * new1
        small = (small - mixing * pltpu.roll(small, 1, 0)) * lax.rsqrt(diag)
        inverse = small[:, BLOCK : 2 * BLOCK]
        panel = nn(inverse, rows, highest)
        out[pl.ds(start, BLOCK), :] = panel[:, width:]
        lanes = iota((BLOCK, width), 1)
        below = jnp.where(lanes >= start + BLOCK, panel[:, :width], 0.0)
        ph, pm, pw = split3(below)
        qh, qm, qw = split3(panel)
        left_side = jnp.concatenate([ph, ph, pm, ph, pw, pm], 0)
        right_side = jnp.concatenate([qh, qm, qh, qw, qh, qm], 0)
        work[...] -= tn(left_side, right_side)
        return carry

    lax.fori_loop(0, width // BLOCK, block_step, 0)


def load_matrix(work, matrix, ridge):
    width = matrix.shape[0]
    eye = jnp.where(iota((width, width), 0) == iota((width, width), 1), 1.0, 0.0)
    if ridge is None:
        ridge = shrink_share * jnp.sum(matrix * eye) / width
    work[:, :width] = matrix + ridge * eye
    work[:, width:] = eye


def leaf_kernel(y_ref, w_ref, work, inv):
    y = y_ref[...]
    width = y.shape[1]
    load_matrix(work, tn(y, y, highest), None)
    inverse_factor(work, inv, width)
    w_ref[...] = nt(inv[...], y, highest).astype(bf16)


def leaf_weights_of(y):
    rows, width = y.shape
    return pl.pallas_call(
        leaf_kernel,
        out_shape=jax.ShapeDtypeStruct((width, rows), bf16),
        in_specs=[VMEM_SPEC],
        out_specs=VMEM_SPEC,
        scratch_shapes=[pltpu.VMEM((width, 2 * width), f32), pltpu.VMEM((width, width), f32)],
    )(y)


def merge_kernel(inner_ridge, g_ref, phi_ref, w_ref, k_ref, work, inv):
    width = phi_ref.shape[1]
    aa, ab, bb = (g_ref[i * width : (i + 1) * width, :] for i in range(3))
    top, low = phi_ref[:width, :], phi_ref[width:, :]
    y_top = nn(aa, top, highest) + nn(ab, low, highest)
    y_low = tn(ab, top, highest) + nn(bb, low, highest)
    load_matrix(work, tn(y_top, y_top, highest) + tn(y_low, y_low, highest), None)
    inverse_factor(work, inv, width)
    w_top = nt(inv[...], y_top, highest)
    w_low = nt(inv[...], y_low, highest)
    w_ref[:, :width] = w_top
    w_ref[:, width:] = w_low
    wg_top = nn(w_top, aa, highest) + nt(w_low, ab, highest)
    wg_low = nn(w_top, ab, highest) + nn(w_low, bb, highest)
    own_gram = nt(wg_top, w_top, highest) + nt(wg_low, w_low, highest)
    if inner_ridge is None:
        k_ref[...] = own_gram
        return
    load_matrix(work, own_gram, inner_ridge)
    inverse_factor(work, inv, width)
    k_ref[...] = tn(inv[...], inv[...], highest)


def merge_weights_of(gram, phi, inner_ridge):
    width = phi.shape[1]
    return pl.pallas_call(
        functools.partial(merge_kernel, inner_ridge),
        out_shape=(
            jax.ShapeDtypeStruct((width, 2 * width), f32),
            jax.ShapeDtypeStruct((width, width), f32),
        ),
        in_specs=[VMEM_SPEC] * 2,
        out_specs=(VMEM_SPEC,) * 2,
        scratch_shapes=[pltpu.VMEM((width, 2 * width), f32), pltpu.VMEM((width, width), f32)],
    )(gram, phi)


def small_sum_kernel(axis, n, x_ref, o_ref, land, send_sem, recv_sem):
    me = lax.axis_index(axis)
    barrier = pltpu.get_barrier_semaphore()
    for d in range(1, n):
        pl.semaphore_signal(barrier, inc=1, device_id={axis: lax.rem(me + d, n)}, device_id_type=MESH)
    pl.semaphore_wait(barrier, n - 1)
    for d in range(1, n):
        pltpu.make_async_remote_copy(
            x_ref, land.at[me], send_sem.at[d], recv_sem.at[me],
            device_id={axis: lax.rem(me + d, n)}, device_id_type=MESH,
        ).start()
    land[me] = x_ref[...]
    for d in range(1, n):
        source = lax.rem(me + n - d, n)
        pltpu.make_async_remote_copy(
            x_ref, land.at[source], send_sem.at[d], recv_sem.at[source],
            device_id={axis: lax.rem(me + d, n)}, device_id_type=MESH,
        ).wait()
    total = land[0]
    for i in range(1, n):
        total = total + land[i]
    o_ref[...] = total


def small_sum(x, axis, collective_id):
    n = lax.axis_size(axis)
    return pl.pallas_call(
        functools.partial(small_sum_kernel, axis, n),
        out_shape=jax.ShapeDtypeStruct(x.shape, f32),
        in_specs=[VMEM_SPEC],
        out_specs=VMEM_SPEC,
        scratch_shapes=[
            pltpu.VMEM((n, *x.shape), f32),
            pltpu.SemaphoreType.DMA((n,)),
            pltpu.SemaphoreType.DMA((n,)),
        ],
        compiler_params=pltpu.CompilerParams(collective_id=collective_id, has_side_effects=True),
    )(x)


def big_sum_kernel(n, share, x_ref, o_ref, land1, out1, land2, full, s1, r1, s2, r2, sa, ra, sb, rb, sc, rc, sd, rd):
    me = lax.axis_index("cols")
    position = lax.axis_index("rows")
    base = position // share * share
    own = lax.rem(position, share)
    side, line, far = lax.rem(me, 2), me // 2, n // 2
    other = 1 - side
    halves = max(share // 2, 1)
    chunk = x_ref.shape[0] // (n * share)

    def rows_of(line_at, side_at, sub):
        return pl.ds(pl.multiple_of((sub * n + line_at * 2 + side_at) * chunk, chunk), chunk)

    def along(t):
        return lax.rem(line + t, far)

    def back(t):
        return lax.rem(line + far - t, far)

    def sub_of(e, mine):
        return lax.rem(mine + share - 2 * e, share)

    pair = {"rows": position, "cols": line * 2 + other}
    sibling = {"rows": base + own + 1 - 2 * lax.rem(own, 2), "cols": me}
    sibling_own = own + 1 - 2 * lax.rem(own, 2)

    def peer(t, e):
        return {"rows": base + lax.rem(own + 2 * e, share), "cols": along(t) * 2 + side}

    spread = [(t, e) for e in range(halves) for t in range(far)]
    greeted = [pair] + [peer(t, e) for t, e in spread if t or e] + ([sibling] if share > 1 else [])
    barrier = pltpu.get_barrier_semaphore()
    for device in greeted:
        pl.semaphore_signal(barrier, inc=1, device_id=device, device_id_type=MESH)
    pl.semaphore_wait(barrier, len(greeted))

    def copy(src, dst, send, recv, device):
        return pltpu.make_async_remote_copy(src, dst, send, recv, device_id=device, device_id_type=MESH)

    first = []
    for t in range(far):
        rows = rows_of(along(t + 1), other, own)
        first.append(copy(x_ref.at[rows], land1.at[t], s1.at[t], r1.at[t], pair))
        first[-1].start()
    second = []
    for t in range(far):
        first[t].wait_recv()
        total = land1[t] + x_ref[rows_of(along(t + 1), side, own), :]
        if t + 1 < far:
            out1[t] = total
            second.append(copy(out1.at[t], land2.at[t], s2.at[t], r2.at[t], peer(t + 1, 0)))
            second[-1].start()
    for t in range(far - 1):
        second[t].wait_recv()
        total = total + land2[t]
    mine = rows_of(line, side, own)
    full[mine, :] = total

    outward, started = {}, []
    for t, e in spread:
        if t or e:
            outward[t, e] = copy(full.at[mine], full.at[mine], sa.at[t, e], ra.at[t, e], peer(t, e))
            outward[t, e].start()
    for t, e in spread:
        rows = rows_of(back(t), side, sub_of(e, own))
        if t or e:
            copy(full.at[mine], full.at[rows], sa.at[t, e], ra.at[t, e], peer(t, e)).wait_recv()
        started.append(copy(full.at[rows], full.at[rows], sb.at[t, e], rb.at[t, e], pair))
        started[-1].start()
        if share > 1:
            started.append(copy(full.at[rows], full.at[rows], sc.at[t, e], rc.at[t, e], sibling))
            started[-1].start()
    for t, e in spread:
        rows = rows_of(back(t), other, sub_of(e, own))
        copy(full.at[rows], full.at[rows], sb.at[t, e], rb.at[t, e], pair).wait_recv()
        if share > 1:
            started.append(copy(full.at[rows], full.at[rows], sd.at[t, e], rd.at[t, e], sibling))
            started[-1].start()
    if share > 1:
        for t, e in spread:
            rows = rows_of(back(t), side, sub_of(e, sibling_own))
            copy(full.at[rows], full.at[rows], sc.at[t, e], rc.at[t, e], sibling).wait_recv()
            rows = rows_of(back(t), other, sub_of(e, sibling_own))
            copy(full.at[rows], full.at[rows], sd.at[t, e], rd.at[t, e], sibling).wait_recv()
    for sent in first + second + list(outward.values()) + started:
        sent.wait_send()
    o_ref[...] = full[...]


def big_sum(x, share, collective_id):
    n = lax.axis_size("cols")
    while share > 1 and x.shape[0] % (n * share * 8):
        share //= 2
    chunk = x.shape[0] // (n * share)
    far, halves = n // 2, max(share // 2, 1)
    dma = pltpu.SemaphoreType.DMA
    return pl.pallas_call(
        functools.partial(big_sum_kernel, n, share),
        out_shape=jax.ShapeDtypeStruct(x.shape, f32),
        in_specs=[VMEM_SPEC],
        out_specs=VMEM_SPEC,
        scratch_shapes=[
            pltpu.VMEM((far, chunk, x.shape[1]), f32),
            pltpu.VMEM((far, chunk, x.shape[1]), f32),
            pltpu.VMEM((far, chunk, x.shape[1]), f32),
            pltpu.VMEM(x.shape, f32),
        ]
        + [dma((far,))] * 4
        + [dma((far, halves))] * 8,
        compiler_params=pltpu.CompilerParams(collective_id=collective_id, has_side_effects=True),
    )(x)


PIECES = 8


def swap_kernel(stride, x_ref, o_ref, land, ss, rs, fs, fr):
    position = lax.axis_index("rows")
    core = lax.rem(position, 2)
    partner = {"rows": position + stride - 2 * stride * lax.rem(position // stride, 2)}
    sibling = {"rows": position + 1 - 2 * core}
    piece = x_ref.shape[0] // (2 * PIECES)
    barrier = pltpu.get_barrier_semaphore()
    for device in (partner, sibling):
        pl.semaphore_signal(barrier, inc=1, device_id=device, device_id_type=MESH)
    pl.semaphore_wait(barrier, 2)

    def rows_of(half, i):
        return pl.ds(pl.multiple_of((half * PIECES + i) * piece, piece), piece)

    sent = []
    for i in range(PIECES):
        rows = rows_of(core, i)
        sent.append(
            pltpu.make_async_remote_copy(
                x_ref.at[rows], land.at[rows], ss.at[i], rs.at[i], device_id=partner, device_id_type=MESH
            )
        )
        sent[-1].start()
    passed = []
    for i in range(PIECES):
        rows = rows_of(core, i)
        sent[i].wait_recv()
        passed.append(
            pltpu.make_async_remote_copy(
                land.at[rows], land.at[rows], fs.at[i], fr.at[i], device_id=sibling, device_id_type=MESH
            )
        )
        passed[-1].start()
    for i in range(PIECES):
        rows = rows_of(1 - core, i)
        pltpu.make_async_remote_copy(
            land.at[rows], land.at[rows], fs.at[i], fr.at[i], device_id=sibling, device_id_type=MESH
        ).wait_recv()
    for copy in sent + passed:
        copy.wait_send()
    o_ref[...] = land[...]


def split_swap(x, stride, collective_id):
    dma = pltpu.SemaphoreType.DMA
    return pl.pallas_call(
        functools.partial(swap_kernel, stride),
        out_shape=jax.ShapeDtypeStruct(x.shape, f32),
        in_specs=[VMEM_SPEC],
        out_specs=VMEM_SPEC,
        scratch_shapes=[pltpu.VMEM(x.shape, f32)] + [dma((PIECES,))] * 4,
        compiler_params=pltpu.CompilerParams(collective_id=collective_id, has_side_effects=True),
    )(x)


def fold(value):
    total = value[:, :LANES]
    for i in range(1, value.shape[1] // LANES):
        total = total + value[:, i * LANES : (i + 1) * LANES]
    return total


def total_of(value):
    return jnp.sum(value, axis=1, keepdims=True)


def three_rows(value):
    wide = jnp.broadcast_to(value, (16, value.shape[1]))
    high = wide.astype(bf16).astype(f32)
    mid = (wide - high).astype(bf16).astype(f32)
    low = wide - high - mid
    sub = iota(wide.shape, 0)
    return jnp.where(sub == 0, high, jnp.where(sub == 1, mid, jnp.where(sub == 2, low, 0.0))).astype(bf16)


def many_rows(value):
    return jnp.broadcast_to(value, (16, value.shape[1])).astype(bf16)


def solve_kernel(
    n_rows, n_cols, samples,
    design, weight, scale, theta, misfit, sketch, kinv, out,
    s3, k3, a_send, a_land, b_send, b_land, c_send, c_land,
    a_ss, a_rs, b_ss, b_rs, c_ss, c_rs,
):
    width = sketch.shape[0]
    here = {"rows": lax.axis_index("rows"), "cols": lax.axis_index("cols")}
    sizes = {"rows": n_rows, "cols": n_cols}

    def peer(axis, d):
        return lax.rem(here[axis] + d, sizes[axis])

    barrier = pltpu.get_barrier_semaphore()
    for axis, n in sizes.items():
        for d in range(1, n):
            pl.semaphore_signal(barrier, inc=1, device_id={axis: peer(axis, d)}, device_id_type=MESH)
    pl.semaphore_wait(barrier, n_rows + n_cols - 2)

    def exchange(axis, value, parity, send, land, ss, rs):
        n, me = sizes[axis], here[axis]
        send[...] = value
        for d in range(1, n):
            pltpu.make_async_remote_copy(
                send, land.at[parity, me], ss.at[d], rs.at[parity, me],
                device_id={axis: peer(axis, d)}, device_id_type=MESH,
            ).start()
        land[parity, me] = value
        for d in range(1, n):
            source = peer(axis, n - d)
            pltpu.make_async_remote_copy(
                send, land.at[parity, source], ss.at[d], rs.at[parity, source],
                device_id={axis: peer(axis, d)}, device_id_type=MESH,
            ).wait()
        total = land[parity, 0]
        for i in range(1, n):
            total = total + land[parity, i]
        return total

    def precondition(vector, parity):
        left = three_rows(vector)
        parts = nt(left, s3[0]) + nt(left, s3[1]) + nt(left, s3[2])
        projected = jnp.sum(parts, axis=0, keepdims=True)
        both = jnp.concatenate([projected, fold(vector * vector)], 1)
        both = exchange("cols", both, parity, c_send, c_land, c_ss, c_rs)
        projected = both[:, :width]
        left = three_rows(projected)
        solved = jnp.sum(nn(left, k3[0]) + nn(left, k3[1]) + nn(left, k3[2]), axis=0, keepdims=True)
        left = three_rows(solved)
        removed = jnp.sum(nn(left, s3[0]) + nn(left, s3[1]) + nn(left, s3[2]), axis=0, keepdims=True)
        agreement = (total_of(both[:, width:]) - total_of(projected * solved)) / damping
        return (vector - removed) / damping, agreement

    def backward(inner, extra, parity):
        part = nn(many_rows(inner), design[...])[:1]
        both = jnp.concatenate([part, extra], 1)
        both = exchange("rows", both, parity, b_send, b_land, b_ss, b_rs)
        return scale[...] * both[:, : part.shape[1]] / samples, total_of(both[:, part.shape[1] :])

    for i, piece in enumerate(split3(sketch[...])):
        s3[i] = piece
    for i, piece in enumerate(split3(kinv[...])):
        k3[i] = piece

    scaled, _ = backward(misfit[...], jnp.zeros((1, LANES), f32), 1)
    residual = scaled + damping * theta[...]
    search, agreement = precondition(residual, 1)

    def advance(turn, search, residual, answer, agreement):
        parity = lax.rem(turn, 2)
        part = nt(many_rows(scale[...] * search), design[...])[:1]
        both = jnp.concatenate([part, fold(search * search)], 1)
        both = exchange("cols", both, parity, a_send, a_land, a_ss, a_rs)
        forward = both[:, : part.shape[1]]
        length = total_of(both[:, part.shape[1] :])
        inner = (weight[...] * forward).astype(bf16).astype(f32)
        product, bending = backward(inner, fold(forward * inner), parity)
        product = product + damping * search
        step_size = agreement / (bending / samples + damping * length)
        return residual - step_size * product, answer + step_size * search

    def body(turn, state):
        search, residual, answer, agreement = state
        residual, answer = advance(turn, search, residual, answer, agreement)
        smoothed, following = precondition(residual, lax.rem(turn, 2))
        return smoothed + following / agreement * search, residual, answer, following

    state = (search, residual, jnp.zeros_like(residual), agreement)
    search, residual, answer, agreement = lax.fori_loop(0, ITERS - 1, body, state)
    _, answer = advance(ITERS - 1, search, residual, answer, agreement)
    out[...] = answer


def solve(design, weight, scale, theta, misfit, sketch, kinv, collective_id):
    rows, cols = design.shape
    width = sketch.shape[0]
    n_rows, n_cols = lax.axis_size("rows"), lax.axis_size("cols")
    dma = pltpu.SemaphoreType.DMA
    return pl.pallas_call(
        functools.partial(solve_kernel, n_rows, n_cols, rows * n_rows),
        out_shape=jax.ShapeDtypeStruct((1, cols), f32),
        in_specs=[VMEM_SPEC] * 7,
        out_specs=VMEM_SPEC,
        scratch_shapes=[
            pltpu.VMEM((3, width, cols), bf16),
            pltpu.VMEM((3, width, width), bf16),
            pltpu.VMEM((1, rows + LANES), f32),
            pltpu.VMEM((2, n_cols, 1, rows + LANES), f32),
            pltpu.VMEM((1, cols + LANES), f32),
            pltpu.VMEM((2, n_rows, 1, cols + LANES), f32),
            pltpu.VMEM((1, width + LANES), f32),
            pltpu.VMEM((2, n_cols, 1, width + LANES), f32),
            dma((n_cols,)), dma((2, n_cols)),
            dma((n_rows,)), dma((2, n_rows)),
            dma((n_cols,)), dma((2, n_cols)),
        ],
        compiler_params=pltpu.CompilerParams(collective_id=collective_id, has_side_effects=True),
    )(design, weight, scale, theta, misfit, sketch, kinv)


def swapped(value, axis, stride):
    mask = 2**stride
    pairs = [(source, source ^ mask) for source in range(lax.axis_size(axis))]
    return lax.ppermute(value, axis, pairs)


def on_device(design, theta, feature_scale, labels, psi, phi):
    row_devices = lax.axis_size("rows")
    samples = design.shape[0] * row_devices
    width = psi.shape[1]
    scaled_theta = (theta * feature_scale).astype(bf16)
    part = jnp.dot(design, scaled_theta, preferred_element_type=f32)
    margins = small_sum(part.reshape(-1, LANES), "cols", 0).reshape(-1)
    chance = jax.nn.sigmoid(margins)
    weight = chance * (1.0 - chance)
    misfit = (chance - labels.astype(f32)).astype(bf16).astype(f32)
    rows_scaled = (
        design.astype(f32) * jnp.sqrt(weight)[:, None] * feature_scale[None, :]
    ).astype(bf16)
    mixed_cols = jnp.einsum("rf,rs->fs", rows_scaled, psi, preferred_element_type=f32).astype(bf16)
    range_rows = big_sum(jnp.dot(rows_scaled, mixed_cols, preferred_element_type=f32), 1, 1)
    sketch = jnp.dot(leaf_weights_of(range_rows), rows_scaled, preferred_element_type=f32)
    position = lax.axis_index("rows")
    levels = row_devices.bit_length() - 1
    features = sketch.shape[1]
    for level_bit in range(levels):
        if level_bit:
            sketch = jnp.concatenate([sketch, own_gram], 1)
            partner = split_swap(sketch, 1 << level_bit, 8 + level_bit)
        else:
            partner = swapped(sketch, "rows", level_bit)
        first_low = position // (1 << level_bit) % 2 == 0
        lower_half = jnp.where(first_low, sketch, partner)
        upper_half = jnp.where(first_low, partner, sketch)
        lower, upper = lower_half[:, :features], upper_half[:, :features]
        gram = jnp.dot(lower, upper.T, precision=highest)
        if level_bit:
            gram = big_sum(gram, 2 << level_bit, 2 + level_bit)
            gram = jnp.concatenate([lower_half[:, features:], gram, upper_half[:, features:]], 0)
        else:
            gram = jnp.concatenate(
                [
                    jnp.dot(lower, lower.T, precision=highest),
                    gram,
                    jnp.dot(upper, upper.T, precision=highest),
                ],
                0,
            )
            gram = big_sum(gram, 2, 2)
        last = level_bit + 1 == levels
        weights, own_gram = merge_weights_of(gram, phi, damping * samples if last else None)
        sketch = jnp.dot(weights, jnp.concatenate([lower, upper], 0), precision=highest)
    answer = solve(
        design, weight[None], feature_scale[None], theta[None], misfit[None], sketch, own_gram, 2 + levels
    )
    return answer[0], sketch


def solution(mesh):
    in_specs = (P("rows", "cols"), P("cols"), P("cols"), P("rows"), P(), P())
    out_specs = (P("cols"), P(None, "cols"))
    return jax.shard_map(
        on_device, mesh=mesh, in_specs=in_specs, out_specs=out_specs, check_vma=False
    )
```

time: 1240 us -> 415 us (0.33)
  blocking collectives: 475 us -> 0 us
  Pallas kernels: 0 us -> 377 us
  waiting for transfers between devices: 298 us -> 2.38 us
  other arithmetic: 259 us -> 9.98 us
  matrix products: 123 us -> 20.8 us
  between operations: 48.3 us -> 0.83 us
  local copies, waits for them, and re-layouts: 32.1 us -> 2.57 us
    psum x32 -> x0, blocking collectives: 475 us -> none  [the longest x10 201 us: on_device(): lax.psum((jnp.dot(design, rounded, preferred_element_type=jnp.float32), j...]
    pallas_call x0 -> x9, Pallas kernels: none -> 377 us  [the longest x1 144 us: solve(): pl.pallas_call(functools.partial(solve_kernel, n_rows, n_cols, rows * n_r...]
    psum x4 -> x0, waiting for transfers between devices: 271 us -> none  [the longest x2 149 us: on_device(): gram = lax.psum(jnp.dot(stacked, stacked.T, precision=highest), 'cols')]
    another operation x46 -> x0, other arithmetic: 223 us -> none  [the longest x20 105 us: shrink_weights(): jnp.linalg.cholesky(moment + ridge * jnp.eye(width, dtype=jnp.float32))]
    dot_general x53 -> x9, matrix products: 87.7 us -> 20.8 us  [the longest x2 6.89 us: on_device(): jnp.dot(weights, jnp.concatenate([lower, upper], 0), precision=highest)]
    another operation x77 -> x0, matrix products: 35.6 us -> none  [the longest x60 23.1 us: precondition_plus(): solved = jax.scipy.linalg.cho_solve((kernel_factor, True), projected)]
    reduce_sum x40 -> x0, other arithmetic: 25.6 us -> none  [the longest x10 6.69 us: on_device(): jnp.sum(forward_rows * inner.astype(jnp.float32))]
    ppermute x2 -> x1, waiting for transfers between devices: 26.7 us -> 2.38 us  [swapped(): return lax.ppermute(value, axis, pairs)]
  transfers between devices with their start and end apart: 6 -> 1, of which waited for: 6 -> 1; matrix products, arithmetic and copies ran while one was open for 0% -> 0% of each run, Pallas kernels for 0% -> 0%
where the time goes in v1:
time: 415 us; the launch traced here: 414 us
  Pallas kernels  377 us (91%)
  matrix products  20.8 us (5%)
  other arithmetic  9.98 us (2%)
    pallas_call x1, Pallas kernels, solve(): pl.pallas_call(functools.partial(solve_kernel, n_rows, n_cols, rows * n_r...  144 us
    pallas_call x2, Pallas kernels, merge_weights_of(): pl.pallas_call(functools.partial(merge_kernel, inner_ridge), out_shape=(j...  90.6 us
    pallas_call x3, Pallas kernels, big_sum(): pl.pallas_call(functools.partial(big_sum_kernel, n, share), out_shape=jax...  82.3 us
    pallas_call x1, Pallas kernels, leaf_weights_of(): pl.pallas_call(leaf_kernel, out_shape=jax.ShapeDtypeStruct((width, rows),...  29.6 us
    pallas_call x1, Pallas kernels, split_swap(): pl.pallas_call(functools.partial(swap_kernel, stride), out_shape=jax.Shap...  20.8 us
    pallas_call x1, Pallas kernels, small_sum(): pl.pallas_call(functools.partial(small_sum_kernel, axis, n), out_shape=ja...  9.8 us
  transfers between devices with their start and end apart: 1, of which 1 were waited for; matrix products, arithmetic and copies ran while one was open for 0% of the time, Pallas kernels for 0%

profile of v1, /device:TPU:0, one launch (start us, length us, event | category | flops | bytes accessed | tf_op | source)
XLA Modules:
  0.0 413.9 jit_solution(7832117728143504641)
XLA Ops:
  0.6 0.0 copy-start
  0.7 0.9 multiply_convert_fusion.4
  1.5 2.8 fusion.18
  4.4 9.8 %shard_map.77 = f32[8,128]{1,0:T(8,128)} custom-call(f32[8,128]{1,0:T(8,128)} %bitcast.30), custom_call_target="tpu_custom_call" | custom-call | tf_op jit(solution)/shard_map/pallas_call | solution.py:182
  14.2 1.3 fusion.10
  15.5 3.3 fusion.8.x_ref
  18.8 37.1 %shard_map.78.y_ref = f32[1024,256]{1,0:T(8,128)} custom-call(f32[1024,256]{1,0:T(8,128)} %fusion.8.x_ref), custom_call_target="tpu_custom_call" | custom-call | tf_op jit(solution)/shard_map/pallas_call | solution.py:292
  56.0 29.6 %shard_map.79 = bf16[256,1024]{1,0:T(8,128)(2,1)} custom-call(f32[1024,256]{1,0:T(8,128)} %shard_map.78.y_ref), custom_call_target="tpu_custom_call" | custom-call | tf_op jit(solution)/shard_map/pallas_call | solution.py:110
  85.6 2.9 fusion.9
  88.4 0.6 subtract_multiply_fusion.1.weight
  89.0 2.4 collective-permute-done
  91.4 1.7 broadcast_select_fusion.3
  93.1 1.0 fusion.19
  94.2 1.0 fusion.20
  95.2 1.0 fusion.21
  96.3 0.9 pad_maximum_fusion.1.x_ref
  97.2 25.6 %shard_map.80.g_ref = f32[768,256]{1,0:T(8,128)} custom-call(f32[768,256]{1,0:T(8,128)} %pad_maximum_fusion.1.x_ref), custom_call_target="tpu_custom_call" | custom-call | tf_op jit(solution)/shard_map/pallas_call | solution.py:292
  122.8 32.6 %shard_map.81 = (f32[256,512]{1,0:T(8,128)}, f32[256,256]{1,0:T(8,128)}) custom-call(f32[768,256]{1,0:T(8,128)} %shard_map.80.g_ref, f32[512,256]{1,0:T(8,128)} %phi_ref.3), custom_call_target="tpu_custom_call" | custom-call | tf_op jit(solution)/shard_map/pallas_call | solution.py:144
  155.4 3.0 fusion
  158.4 1.0 copy-done.1
  159.3 1.2 pad_maximum_fusion.x_ref
  160.5 20.8 %shard_map.82 = f32[256,1280]{1,0:T(8,128)} custom-call(f32[256,1280]{1,0:T(8,128)} %pad_maximum_fusion.x_ref), custom_call_target="tpu_custom_call" | custom-call | tf_op jit(solution)/shard_map/pallas_call | solution.py:357
  181.3 1.5 broadcast_select_fusion.1
  182.9 0.1 slice.17
  183.0 1.7 fusion.15.x_ref
  184.8 0.1 slice.18
  184.9 19.6 %shard_map.83 = f32[256,256]{1,0:T(8,128)} custom-call(f32[256,256]{1,0:T(8,128)} %fusion.15.x_ref), custom_call_target="tpu_custom_call" | custom-call | tf_op jit(solution)/shard_map/pallas_call | solution.py:292
  204.5 1.9 pad_maximum_fusion.2.g_ref
  206.3 58.0 %shard_map.84 = (f32[256,512]{1,0:T(8,128)}, f32[256,256]{1,0:T(8,128)}) custom-call(f32[768,256]{1,0:T(8,128)} %pad_maximum_fusion.2.g_ref, f32[512,256]{1,0:T(8,128)} %phi_ref.3), custom_call_target="tpu_custom_call" | custom-call | tf_op jit(solution)/shard_map/pallas_call | solution.py:144
  264.4 3.9 fusion.4.sketch
  268.3 144.3 %shard_map.85 = f32[1,1024]{1,0:T(1,128)} custom-call(bf16[1024,1024]{1,0:T(8,128)(2,1)} %design.1, f32[1,1024]{1,0:T(1,128)} %subtract_multiply_fusion.1.weight, f32[1,1024]{1,0:T(1,128)} %bitcast.28, f32[1,1024]{1,0:T(1,128)} %bitcast.27, f32[1,1024]{1,0:T(1,128)} %bitcast.31, f32[256,1024]{1,0:T(8,128)} %fusion.4.sketch, f32[256,256]{1,0:T(8,128)} %get-tuple-element.9.kinv), custom_call_target="tpu_custom_call" | custom-call | tf_op jit(solution)/shard_map/pallas_call | solution.py:489
  412.6 1.3 copy.9
  (19 shorter events, 0.1 us)
Async XLA Ops:
  0.6 14.9 %copy-start = (bf16[1024,256]{1,0:T(8,128)(2,1)S(1)}, bf16[1024,256]{1,0:T(8,128)(2,1)}, u32[]{:S(2)}) copy-start(bf16[1024,256]{1,0:T(8,128)(2,1)} %param.10) | copy-start | bytes 1572868
  0.6 14.8 %copy-start.6 = (f32[1024]{0:T(1024)S(1)}, f32[1024]{0:T(1024)}, u32[]{:S(2)}) copy-start(f32[1024]{0:T(1024)} %param.8) | copy-start | bytes 12292
  0.7 14.8 %copy-start.3 = (bf16[1024,1024]{1,0:T(8,128)(2,1)S(1)}, bf16[1024,1024]{1,0:T(8,128)(2,1)}, u32[]{:S(2)}) copy-start(bf16[1024,1024]{1,0:T(8,128)(2,1)} %design.1) | copy-start | bytes 6291460
  0.7 13.5 %copy-start.7 = (s32[1024]{0:T(1024)S(1)}, s32[1024]{0:T(1024)}, u32[]{:S(2)}) copy-start(s32[1024]{0:T(1024)} %param.9) | copy-start | bytes 12292
  85.6 2.9 copy-start.5
  88.4 3.0 collective-permute-start
  155.4 4.0 copy-start.4
  158.4 1.0 copy-start.1
  160.5 20.8 %copy-start.2 = (f32[256,1024]{1,0:T(8,128)S(1)}, f32[256,1024]{1,0:T(8,128)}, u32[]{:S(2)}) copy-start(f32[256,1024]{1,0:T(8,128)} %copy-done.1) | copy-start | bytes 3145732

commit v2 on v1

--- a/solution.py
+++ b/solution.py
@@ -8,7 +8,7 @@
 from jax.sharding import PartitionSpec as P
 
 ITERS = 10
-BLOCK = 32
+BLOCK = 64
 LANES = 128
 
 damping = 0.01
@@ -53,26 +53,42 @@
         lane = iota((BLOCK, LANES), 1)
         sub = iota((BLOCK, LANES), 0)
         small = jnp.where(lane < BLOCK, shifted, jnp.where(lane == sub + BLOCK, 1.0, 0.0))
-        diag = jnp.ones((BLOCK, 1), f32)
-        mixing = jnp.zeros((BLOCK, 1), f32)
-        sub1 = iota((BLOCK, 1), 0)
+        tiles = [small[i : i + 8] for i in range(0, BLOCK, 8)]
+        sub8 = iota((8, LANES), 0)
+        diags, mixings = [], []
         for j in range(0, BLOCK, 2):
-            col0, col1 = small[:, j : j + 1], small[:, j + 1 : j + 2]
-            row0, row1 = small[j : j + 1, :], small[j + 1 : j + 2, :]
-            p00 = small[j : j + 1, j : j + 1]
-            p01 = small[j : j + 1, j + 1 : j + 2]
-            p11 = small[j + 1 : j + 2, j + 1 : j + 2]
+            at, r = j // 8, j % 8
+            if r == 0:
+                diag = jnp.ones((8, LANES), f32)
+                mixing = jnp.zeros((8, LANES), f32)
+            wide0 = [jnp.broadcast_to(tile[:, j : j + 1], (8, LANES)) for tile in tiles[at:]]
+            wide1 = [jnp.broadcast_to(tile[:, j + 1 : j + 2], (8, LANES)) for tile in tiles[at:]]
+            row0, row1 = (jnp.broadcast_to(tiles[at][r + i : r + i + 1], (8, LANES)) for i in range(2))
+            p00 = jnp.broadcast_to(wide0[0][r : r + 1], (8, LANES))
+            p01 = jnp.broadcast_to(wide0[0][r + 1 : r + 2], (8, LANES))
+            p11 = jnp.broadcast_to(wide1[0][r + 1 : r + 2], (8, LANES))
             det = p00 * p11 - p01 * p01
-            diag = jnp.where(sub1 == j, p00, jnp.where(sub1 == j + 1, det / p00, diag))
-            mixing = jnp.where(sub1 == j + 1, p01 / p00, mixing)
+            ratio = 1.0 / p00
+            diag = jnp.where(sub8 == r, p00, jnp.where(sub8 == r + 1, det * ratio, diag))
+            mixing = jnp.where(sub8 == r + 1, p01 * ratio, mixing)
+            if r == 6:
+                diags.append(diag)
+                mixings.append(mixing)
             if j + 2 < BLOCK:
                 share = 1.0 / det
                 new0 = (p11 * row0 - p01 * row1) * share
                 new1 = (p00 * row1 - p01 * row0) * share
-                below0 = jnp.where(sub1 > j + 1, col0, 0.0)
-                below1 = jnp.where(sub1 > j + 1, col1, 0.0)
-                small = small - below0 * new0 - below1 * new1
-        small = (small - mixing * pltpu.roll(small, 1, 0)) * lax.rsqrt(diag)
+                wide0[0] = jnp.where(sub8 > r + 1, wide0[0], 0.0)
+                wide1[0] = jnp.where(sub8 > r + 1, wide1[0], 0.0)
+                for i in range(at, len(tiles)):
+                    tiles[i] = tiles[i] - (wide0[i - at] * new0 + wide1[i - at] * new1)
+        small = jnp.concatenate(
+            [
+                (tile - mixing * pltpu.roll(tile, 1, 0)) * lax.rsqrt(diag)
+                for tile, diag, mixing in zip(tiles, diags, mixings)
+            ],
+            0,
+        )
         inverse = small[:, BLOCK : 2 * BLOCK]
         panel = nn(inverse, rows, highest)
         out[pl.ds(start, BLOCK), :] = panel[:, width:]

time: 415 us -> 393 us (0.947)
  Pallas kernels: 377 us -> 356 us
    pallas_call x2, Pallas kernels: 90.6 us -> 74.6 us  [merge_weights_of(): pl.pallas_call(functools.partial(merge_kernel, inner_ridge), out_shape=(j...]
    pallas_call x1, Pallas kernels: 29.6 us -> 24.3 us  [leaf_weights_of(): pl.pallas_call(leaf_kernel, out_shape=jax.ShapeDtypeStruct((width, rows),...]
where the time goes in v2:
time: 393 us
  Pallas kernels  356 us (91%)
  matrix products  20.8 us (5%)
  other arithmetic  9.98 us (3%)
    pallas_call x1, Pallas kernels, solve(): pl.pallas_call(functools.partial(solve_kernel, n_rows, n_cols, rows * n_r...  144 us
    pallas_call x3, Pallas kernels, big_sum(): pl.pallas_call(functools.partial(big_sum_kernel, n, share), out_shape=jax...  82.2 us
    pallas_call x2, Pallas kernels, merge_weights_of(): pl.pallas_call(functools.partial(merge_kernel, inner_ridge), out_shape=(j...  74.6 us
    pallas_call x1, Pallas kernels, leaf_weights_of(): pl.pallas_call(leaf_kernel, out_shape=jax.ShapeDtypeStruct((width, rows),...  24.3 us
    pallas_call x1, Pallas kernels, split_swap(): pl.pallas_call(functools.partial(swap_kernel, stride), out_shape=jax.Shap...  20.8 us
    pallas_call x1, Pallas kernels, small_sum(): pl.pallas_call(functools.partial(small_sum_kernel, axis, n), out_shape=ja...  9.8 us
  transfers between devices with their start and end apart: 1, of which 1 were waited for; matrix products, arithmetic and copies ran while one was open for 0% of the time, Pallas kernels for 0%

profile of v2, /device:TPU:0, one launch (start us, length us, event | category | flops | bytes accessed | tf_op | source)
XLA Modules:
  0.0 392.6 jit_solution(2824433316227864516)
XLA Ops:
  0.6 0.0 copy-start
  0.7 0.9 multiply_convert_fusion.4
  1.5 2.8 fusion.18
  4.4 9.8 %shard_map.77 = f32[8,128]{1,0:T(8,128)} custom-call(f32[8,128]{1,0:T(8,128)} %bitcast.30), custom_call_target="tpu_custom_call" | custom-call | tf_op jit(solution)/shard_map/pallas_call | solution.py:198
  14.2 1.3 fusion.10
  15.5 3.3 fusion.8.x_ref
  18.8 37.1 %shard_map.78.y_ref = f32[1024,256]{1,0:T(8,128)} custom-call(f32[1024,256]{1,0:T(8,128)} %fusion.8.x_ref), custom_call_target="tpu_custom_call" | custom-call | tf_op jit(solution)/shard_map/pallas_call | solution.py:308
  56.0 24.3 %shard_map.79 = bf16[256,1024]{1,0:T(8,128)(2,1)} custom-call(f32[1024,256]{1,0:T(8,128)} %shard_map.78.y_ref), custom_call_target="tpu_custom_call" | custom-call | tf_op jit(solution)/shard_map/pallas_call | solution.py:126
  80.2 2.9 fusion.9
  83.1 0.6 subtract_multiply_fusion.1.weight
  83.7 2.4 collective-permute-done
  86.1 1.7 broadcast_select_fusion.3
  87.8 1.0 fusion.19
  88.9 1.0 fusion.20
  89.9 1.0 fusion.21
  90.9 0.9 pad_maximum_fusion.1.x_ref
  91.9 25.5 %shard_map.80.g_ref = f32[768,256]{1,0:T(8,128)} custom-call(f32[768,256]{1,0:T(8,128)} %pad_maximum_fusion.1.x_ref), custom_call_target="tpu_custom_call" | custom-call | tf_op jit(solution)/shard_map/pallas_call | solution.py:308
  117.4 27.3 %shard_map.81 = (f32[256,512]{1,0:T(8,128)}, f32[256,256]{1,0:T(8,128)}) custom-call(f32[768,256]{1,0:T(8,128)} %shard_map.80.g_ref, f32[512,256]{1,0:T(8,128)} %phi_ref.3), custom_call_target="tpu_custom_call" | custom-call | tf_op jit(solution)/shard_map/pallas_call | solution.py:160
  144.7 3.0 fusion
  147.7 1.0 copy-done.1
  148.7 1.2 pad_maximum_fusion.x_ref
  149.8 20.8 %shard_map.82 = f32[256,1280]{1,0:T(8,128)} custom-call(f32[256,1280]{1,0:T(8,128)} %pad_maximum_fusion.x_ref), custom_call_target="tpu_custom_call" | custom-call | tf_op jit(solution)/shard_map/pallas_call | solution.py:373
  170.6 1.5 broadcast_select_fusion.1
  172.2 0.1 slice.17
  172.3 1.7 fusion.15.x_ref
  174.1 0.1 slice.18
  174.2 19.6 %shard_map.83 = f32[256,256]{1,0:T(8,128)} custom-call(f32[256,256]{1,0:T(8,128)} %fusion.15.x_ref), custom_call_target="tpu_custom_call" | custom-call | tf_op jit(solution)/shard_map/pallas_call | solution.py:308
  193.8 1.9 pad_maximum_fusion.2.g_ref
  195.7 47.4 %shard_map.84 = (f32[256,512]{1,0:T(8,128)}, f32[256,256]{1,0:T(8,128)}) custom-call(f32[768,256]{1,0:T(8,128)} %pad_maximum_fusion.2.g_ref, f32[512,256]{1,0:T(8,128)} %phi_ref.3), custom_call_target="tpu_custom_call" | custom-call | tf_op jit(solution)/shard_map/pallas_call | solution.py:160
  243.1 3.9 fusion.4.sketch
  247.0 144.3 %shard_map.85 = f32[1,1024]{1,0:T(1,128)} custom-call(bf16[1024,1024]{1,0:T(8,128)(2,1)} %design.1, f32[1,1024]{1,0:T(1,128)} %subtract_multiply_fusion.1.weight, f32[1,1024]{1,0:T(1,128)} %bitcast.28, f32[1,1024]{1,0:T(1,128)} %bitcast.27, f32[1,1024]{1,0:T(1,128)} %bitcast.31, f32[256,1024]{1,0:T(8,128)} %fusion.4.sketch, f32[256,256]{1,0:T(8,128)} %get-tuple-element.9.kinv), custom_call_target="tpu_custom_call" | custom-call | tf_op jit(solution)/shard_map/pallas_call | solution.py:505
  391.3 1.3 copy.9
  (19 shorter events, 0.1 us)
Async XLA Ops:
  0.6 14.9 %copy-start = (bf16[1024,256]{1,0:T(8,128)(2,1)S(1)}, bf16[1024,256]{1,0:T(8,128)(2,1)}, u32[]{:S(2)}) copy-start(bf16[1024,256]{1,0:T(8,128)(2,1)} %param.10) | copy-start | bytes 1572868
  0.6 14.8 %copy-start.6 = (f32[1024]{0:T(1024)S(1)}, f32[1024]{0:T(1024)}, u32[]{:S(2)}) copy-start(f32[1024]{0:T(1024)} %param.8) | copy-start | bytes 12292
  0.7 14.8 %copy-start.3 = (bf16[1024,1024]{1,0:T(8,128)(2,1)S(1)}, bf16[1024,1024]{1,0:T(8,128)(2,1)}, u32[]{:S(2)}) copy-start(bf16[1024,1024]{1,0:T(8,128)(2,1)} %design.1) | copy-start | bytes 6291460
  0.7 13.5 %copy-start.7 = (s32[1024]{0:T(1024)S(1)}, s32[1024]{0:T(1024)}, u32[]{:S(2)}) copy-start(s32[1024]{0:T(1024)} %param.9) | copy-start | bytes 12292
  80.2 2.9 copy-start.5
  83.1 3.0 collective-permute-start
  144.7 4.0 %copy-start.4 = (f32[256,256]{1,0:T(8,128)S(1)}, f32[256,256]{1,0:T(8,128)}, u32[]{:S(2)}) copy-start(f32[256,256]{1,0:T(8,128)} %get-tuple-element.7) | copy-start | bytes 786436
  147.7 1.0 copy-start.1
  149.8 20.8 %copy-start.2 = (f32[256,1024]{1,0:T(8,128)S(1)}, f32[256,1024]{1,0:T(8,128)}, u32[]{:S(2)}) copy-start(f32[256,1024]{1,0:T(8,128)} %copy-done.1) | copy-start | bytes 3145732
